TPU v7x, 32 devices: a whole 2x2x4 slice. The times are simulated.
32 devices in a mesh: dp: 16 (over z, y, x), head: 2 (over core).
Axes of the slice: x: 2, y: 2, z: 4, core: 2. Of those that a mesh axis runs over, the one named last changes fastest.
Arguments:
- teacher_hidden: bfloat16 [40960, 1024], P('dp', 'head'), may hold values from -6 to 6
- student_hidden: bfloat16 [40960, 312], P('dp'), may hold values from -6 to 6
- projector: bfloat16 [312, 1024], P(None, 'head'), may hold values from -0.3125 to 0.3125
- teacher_queries: bfloat16 [40960, 1024], P('dp', 'head'), may hold values from -6 to 6
- teacher_keys: bfloat16 [40960, 1024], P('dp', 'head'), may hold values from -6 to 6
- student_queries: bfloat16 [40960, 312], P('dp', 'head'), may hold values from -6 to 6
- student_keys: bfloat16 [40960, 312], P('dp', 'head'), may hold values from -6 to 6
- lengths: int32 [80], replicated, may hold values from 32 to 512, as said below
- plan: int32 [4, 16], replicated, may hold values from 0 to 4, as said below
Outputs:
- hidden_row: float32 [40960], P(('dp', 'head'))
- row_loss: float32 [16, 2, 5, 256], P('dp', 'head')
- loss: float32 [], replicated
Inputs may be any that keep to these rules, and one draw needn't show every extreme that they name: lengths[k] counts the real tokens of the sequence in rows k * 512 onward, first held in slot k mod 5 of dp index k // 5; the rows after them are padding. Some sequence has exactly 512 tokens. In round r, dp index d gives the sequence in its slot plan[r, d] to dp index d XOR 2^r and receives that device's slot plan[r, d XOR 2^r] into the same slot; the rounds tend to even out the sum of squared lengths of the devices.
All inputs are finite; a program needn't handle non-finite values.
Results may differ from a plain program's by a relative error of at most 0.0003.
Values may be sent and summed in bfloat16 or wider, within the bound.
A program may use at most 128 MiB of HBM per device.

v0:
```python
import math

import jax
import jax.numpy as jnp
from jax import lax
from jax.sharding import PartitionSpec as P

HEADS_T = 16
HEAD_T = 64
HEADS_S = 12
HEAD_S = 26
MAXLEN = 512
D_T = 1024


def partner(value, axis, distance):
    mask = 2**distance
    pairs = [(source, source ^ mask) for source in range(lax.axis_size(axis))]
    return lax.ppermute(value, axis, pairs)


def select_entry(values, my_index):
    picked = jnp.where(jnp.arange(values.shape[0], dtype=jnp.int32) == my_index, values, 0)
    return jnp.sum(picked)


def select_row(slot_table, my_index):
    picked = jnp.where(
        (jnp.arange(slot_table.shape[0], dtype=jnp.int32) == my_index)[:, None], slot_table, 0
    )
    return jnp.sum(picked, axis=0)


def slot_map(operands, length):
    max_rows = operands[0].shape[0]
    tile_rows = max_rows // 4
    t_scale = 1.0 / (HEADS_T * math.sqrt(HEAD_T))
    s_scale = 1.0 / (HEADS_S * math.sqrt(HEAD_S))

    def make_branch(used_rows):

        def branch(values):
            teach_query, teach_key, pupil_query, pupil_key = values
            teacher_map = jnp.einsum(
                "ic,jc->ij",
                teach_query[:used_rows],
                teach_key[:used_rows],
                preferred_element_type=jnp.float32,
            )
            student_map = jnp.einsum(
                "ic,jc->ij",
                pupil_query[:used_rows],
                pupil_key[:used_rows],
                preferred_element_type=jnp.float32,
            )
            inside = jnp.arange(used_rows, dtype=jnp.int32) < length
            difference = jnp.where(
                inside[:, None] & inside[None, :],
                teacher_map * t_scale - student_map * s_scale,
                0.0,
            )
            return jnp.pad(difference, ((0, max_rows - used_rows), (0, max_rows - used_rows)))

        return branch

    branches = [make_branch((bucket + 1) * tile_rows) for bucket in range(4)]
    bucket_index = (length + tile_rows - 1) // tile_rows - 1
    return lax.switch(bucket_index, branches, operands)


def attention_rows(pieces, slot_lengths):
    slot_count = pieces[0].shape[0]
    full_maps = jnp.stack(
        [
            slot_map(tuple((member[slot_number] for member in pieces)), slot_lengths[slot_number])
            for slot_number in range(slot_count)
        ]
    )
    halves = lax.psum_scatter(full_maps, "head", scatter_dimension=1, tiled=True)
    squares = halves * halves
    row_losses = jnp.sum(squares, axis=2) / slot_lengths[:, None].astype(jnp.float32)
    return (row_losses, jnp.sum(squares))


def body(
    teacher_hidden,
    student_hidden,
    projector,
    teacher_queries,
    teacher_keys,
    student_queries,
    student_keys,
    lengths,
    plan,
):
    device_count = lax.axis_size("dp")
    my_index = lax.axis_index("dp")
    slot_count = teacher_hidden.shape[0] // MAXLEN
    slot_table = lengths.reshape(device_count, slot_count)
    own_lengths = select_row(slot_table, my_index)
    projected = jnp.dot(student_hidden, projector, preferred_element_type=jnp.float32)
    errors = projected - teacher_hidden.astype(jnp.float32)
    row_part = jnp.sum(errors * errors, axis=1).reshape(slot_count, MAXLEN)
    inside = jnp.arange(MAXLEN, dtype=jnp.int32)[None, :] < own_lengths[:, None]
    row_part = jnp.where(inside, row_part, 0.0).reshape(slot_count * MAXLEN)
    hidden_row = lax.psum_scatter(row_part, "head", scatter_dimension=0, tiled=True) / D_T
    hidden_local = jnp.sum(hidden_row)
    pieces = (
        teacher_queries.reshape(slot_count, MAXLEN, -1),
        teacher_keys.reshape(slot_count, MAXLEN, -1),
        student_queries.reshape(slot_count, MAXLEN, -1),
        student_keys.reshape(slot_count, MAXLEN, -1),
    )
    row_losses, attention_local = attention_rows(pieces, own_lengths)
    for bit_index in range(plan.shape[0]):
        my_slot = select_entry(plan[bit_index], my_index)
        outgoing = lax.dynamic_index_in_dim(row_losses, my_slot, 0, keepdims=False)
        arrived = partner(outgoing, "dp", bit_index)
        row_losses = lax.dynamic_update_index_in_dim(row_losses, arrived, my_slot, 0)
    hidden_total, attention_total = lax.psum((hidden_local, attention_local), ("dp", "head"))
    lengths_float = lengths.astype(jnp.float32)
    loss = hidden_total / jnp.sum(lengths_float) + attention_total / jnp.sum(
        lengths_float * lengths_float
    )
    return (hidden_row, row_losses.reshape(1, 1, slot_count, row_losses.shape[1]), loss)


def solution(mesh):
    placed = (
        P("dp", "head"),
        P("dp", None),
        P(None, "head"),
        P("dp", "head"),
        P("dp", "head"),
        P("dp", "head"),
        P("dp", "head"),
        P(),
        P(),
    )
    return jax.shard_map(
        body,
        mesh=mesh,
        in_specs=placed,
        out_specs=(P(("dp", "head")), P("dp", "head", None, None), P()),
        check_vma=False,
    )
```

profile of v0, /device:TPU:0, one launch (start us, length us, event | category | flops | bytes accessed | tf_op | source)
XLA Modules:
  0.0 149.4 jit_solution(5598412386411818364)
XLA Ops:
  12.0 8.6 %conditional.5 = (f32[1,512,512]{2,1,0:T(8,128)}) conditional(s32[]{:T(128)} %clamp.15, (s32[]{:T(128)}, bf16[2560,512]{1,0:T(8,128)(2,1)}, bf16[2560,512]{1,0:T(8,128)(2,1)}, bf16[2560,156]{0,1:T(8,128)(2,1)}, bf16[2560,156]{0,1:T(8,128)(2,1)}) %tuple.88, (s32[]{:T(128)}, bf16[2560,512]{1,0:T(8,128)(2,1)}, ...), branch_computations={%region_3.4_spmd, %region_4.5_spmd, %region_5.6_spmd, %region_6.7_... | conditional | flops 351535616 | bytes 11109928 | solution.py:68
  12.1 2.4 %copy.101 = bf16[2560,156]{1,0:T(8,128)(2,1)} copy(bf16[2560,156]{0,1:T(8,128)(2,1)} %get-tuple-element.631) | data formatting | bytes 1597440 | tf_op jit(solution)/shard_map
  14.5 1.4 copy.102
  17.9 2.7 %fusion.20 = f32[1,512,512]{2,1,0:T(8,128)} fusion(f32[512,512]{1,0:T(8,128)S(1)} %convolution_multiply_fusion.7, bf16[2560,512]{1,0:T(8,128)(2,1)} %get-tuple-element.327, bf16[2560,512]{1,0:T(8,128)(2,1)} %get-tuple-element.326, pred[512]{0:T(512)(128)(4,1)S(1)} %iota_compare_fusion.3), kind=kOutput, calls=%fused_computation.33 | convolution fusion | flops 269484032 | bytes 3146752 | tf_op jit(solution)/shard_map/cond/branch_3_fun/ic,jc->ij/dot_general | solution.py:44
  20.6 2.4 %constant_dynamic-update-slice_fusion.4 = f32[5,512,512]{2,1,0:T(8,128)} fusion(f32[1,512,512]{2,1,0:T(8,128)} %get-tuple-element.730), kind=kLoop, calls=%fused_computation.208 | loop fusion | bytes 2097152
  23.0 7.4 %conditional.6 = (f32[1,512,512]{2,1,0:T(8,128)}) conditional(s32[]{:T(128)} %clamp.16, (s32[]{:T(128)}, bf16[2560,512]{1,0:T(8,128)(2,1)}, bf16[2560,512]{1,0:T(8,128)(2,1)}, bf16[2560,156]{0,1:T(8,128)(2,1)S(1)}, bf16[2560,156]{0,1:T(8,128)(2,1)S(1)}) %tuple.202, (s32[]{:T(128)}, bf16[2560,512]{1,0:T(8,128)(2,1)}, ...), branch_computations={%region_7.8_spmd, %region_8.9_spmd, %region_9.10_spmd, %region_10.... | conditional | flops 351535616 | bytes 7915020 | solution.py:68
  23.0 1.4 copy.109
  24.4 1.4 copy.110
  27.7 2.7 %fusion.45 = f32[1,512,512]{2,1,0:T(8,128)} fusion(f32[512,512]{1,0:T(8,128)S(1)} %convolution_multiply_fusion.15, bf16[2560,512]{1,0:T(8,128)(2,1)} %get-tuple-element.347, bf16[2560,512]{1,0:T(8,128)(2,1)} %get-tuple-element.346, pred[512]{0:T(512)(128)(4,1)S(1)} %iota_compare_fusion.7), kind=kOutput, calls=%fused_computation.73 | convolution fusion | flops 269484032 | bytes 3146752 | tf_op jit(solution)/shard_map/cond/branch_3_fun/ic,jc->ij/dot_general | solution.py:44
  30.4 2.3 %constant_dynamic-update-slice_fusion.3 = f32[5,512,512]{2,1,0:T(8,128)} fusion(f32[5,512,512]{2,1,0:T(8,128)} %constant_dynamic-update-slice_fusion.4, f32[1,512,512]{2,1,0:T(8,128)} %get-tuple-element.731), kind=kLoop, calls=%fused_computation.207 | loop fusion | bytes 2097152
  32.7 7.4 %conditional.7 = (f32[1,512,512]{2,1,0:T(8,128)}) conditional(s32[]{:T(128)} %clamp.17, (s32[]{:T(128)}, bf16[2560,512]{1,0:T(8,128)(2,1)}, bf16[2560,512]{1,0:T(8,128)(2,1)}, bf16[2560,156]{0,1:T(8,128)(2,1)S(1)}, bf16[2560,156]{0,1:T(8,128)(2,1)S(1)}) %tuple.206, (s32[]{:T(128)}, bf16[2560,512]{1,0:T(8,128)(2,1)}, ...), branch_computations={%region_11.12_spmd, %region_12.13_spmd, %region_13.14_spmd, %regio... | conditional | flops 351535616 | bytes 7915020 | solution.py:68
  32.7 1.4 copy.115
  34.1 1.4 copy.116
  35.5 1.5 %convolution_multiply_fusion.21 = f32[384,384]{1,0:T(8,128)S(1)} fusion(bf16[2560,512]{1,0:T(8,128)(2,1)} %get-tuple-element.362, bf16[2560,512]{1,0:T(8,128)(2,1)} %get-tuple-element.361), kind=kOutput, calls=%fused_computation.103 | convolution fusion | flops 151142400 | bytes 1376256 | tf_op jit(solution)/shard_map/cond/branch_2_fun/ic,jc->ij/dot_general | solution.py:44
  40.1 2.3 %constant_dynamic-update-slice_fusion.2 = f32[5,512,512]{2,1,0:T(8,128)} fusion(f32[5,512,512]{2,1,0:T(8,128)} %constant_dynamic-update-slice_fusion.3, f32[1,512,512]{2,1,0:T(8,128)} %get-tuple-element.732), kind=kLoop, calls=%fused_computation.206 | loop fusion | bytes 2097152
  42.4 7.5 %conditional.8 = (f32[1,512,512]{2,1,0:T(8,128)}) conditional(s32[]{:T(128)} %clamp.18, (s32[]{:T(128)}, bf16[2560,512]{1,0:T(8,128)(2,1)}, bf16[2560,512]{1,0:T(8,128)(2,1)}, bf16[2560,156]{0,1:T(8,128)(2,1)S(1)}, bf16[2560,156]{0,1:T(8,128)(2,1)S(1)}) %tuple.210, (s32[]{:T(128)}, bf16[2560,512]{1,0:T(8,128)(2,1)}, ...), branch_computations={%region_15.16_spmd, %region_16.17_spmd, %region_17.18_spmd, %regio... | conditional | flops 351535616 | bytes 7915020 | solution.py:68
  43.8 1.4 copy.126
  47.2 2.7 %fusion.95 = f32[1,512,512]{2,1,0:T(8,128)} fusion(f32[512,512]{1,0:T(8,128)S(1)} %convolution_multiply_fusion.31, bf16[2560,512]{1,0:T(8,128)(2,1)} %get-tuple-element.387, bf16[2560,512]{1,0:T(8,128)(2,1)} %get-tuple-element.386, pred[512]{0:T(512)(128)(4,1)S(1)} %iota_compare_fusion.15), kind=kOutput, calls=%fused_computation.153 | convolution fusion | flops 269484032 | bytes 3146752 | tf_op jit(solution)/shard_map/cond/branch_3_fun/ic,jc->ij/dot_general | solution.py:44
  49.9 2.3 %constant_dynamic-update-slice_fusion.1 = f32[5,512,512]{2,1,0:T(8,128)} fusion(f32[5,512,512]{2,1,0:T(8,128)} %constant_dynamic-update-slice_fusion.2, f32[1,512,512]{2,1,0:T(8,128)} %get-tuple-element.733), kind=kLoop, calls=%fused_computation.205 | loop fusion | bytes 2097152
  52.2 7.1 %conditional.9 = (f32[1,512,512]{2,1,0:T(8,128)}) conditional(s32[]{:T(128)} %clamp.19, (s32[]{:T(128)}, bf16[2560,512]{1,0:T(8,128)(2,1)}, bf16[2560,512]{1,0:T(8,128)(2,1)}, bf16[2560,156]{0,1:T(8,128)(2,1)S(1)}, bf16[2560,156]{0,1:T(8,128)(2,1)S(1)}) %tuple.214, (s32[]{:T(128)}, bf16[2560,512]{1,0:T(8,128)(2,1)}, ...), branch_computations={%region_19.20_spmd, %region_20.21_spmd, %region_21.22_spmd, %regio... | conditional | flops 351535616 | bytes 7915020 | solution.py:68
  53.6 1.4 copy.130
  59.3 2.3 %constant_dynamic-update-slice_fusion = f32[5,512,512]{2,1,0:T(8,128)} fusion(f32[5,512,512]{2,1,0:T(8,128)} %constant_dynamic-update-slice_fusion.1, f32[1,512,512]{2,1,0:T(8,128)} %get-tuple-element.734), kind=kLoop, calls=%fused_computation.204 | loop fusion | bytes 2097152 | tf_op jit(solution)/shard_map/stack | solution.py:73
  61.7 4.5 %copy.94 = bf16[2560,512]{0,1:T(8,128)(2,1)} copy(bf16[2560,512]{1,0:T(8,128)(2,1)} %param.29) | data formatting | bytes 5242880 | tf_op args[0]
  68.8 4.2 %multiply_reduce_fusion = f32[2560]{0:T(1024)S(1)} fusion(bf16[2560,512]{0,1:T(8,128)(2,1)} %copy.94, bf16[2560,312]{0,1:T(8,128)(2,1)S(1)} %copy-done, bf16[312,512]{1,0:T(8,128)(2,1)S(1)} %copy-done.10), kind=kOutput, calls=%fused_computation.200 | convolution fusion | flops 823129600 | bytes 4548608 | tf_op jit(solution)/shard_map/dot_general | solution.py:101
  73.1 3.5 %reduce-scatter.2.cloned.1.call-done = f32[5,256,512]{2,1,0:T(8,128)} async-done(((f32[5,512,512]{2,1,0:T(8,128)}), f32[5,256,512]{2,1,0:T(8,128)}) %reduce-scatter.2.cloned.1.call-update) | async-done | bytes 2621456 | tf_op jit(solution)/shard_map/reduce_scatter | solution.py:79
  76.6 3.1 %multiply_reduce_fusion.1 = (f32[]{:T(128)}, f32[5,256]{1,0:T(8,128)S(1)}) fusion(f32[5,256,512]{2,1,0:T(8,128)} %reduce-scatter.2.cloned.1.call-done), kind=kLoop, calls=%fused_computation.201 | loop fusion | flops 1964799 | bytes 2626564 | tf_op jit(solution)/shard_map/reduce_sum | solution.py:82
  79.8 1.8 %collective-permute-start = (f32[256]{0:T(256)S(1)}, f32[256]{0:T(256)S(1)}, u32[]{:S(2)}, u32[]{:S(2)}) collective-permute-start(f32[256]{0:T(256)S(1)} %bitcast.79), channel_id=1, source_target_pairs={{0,2},{2,0},{4,6},{6,4},{8,10},{10,8},{12,14},{14,12},{16,18},{18,... | collective-permute-start | bytes 3080 | tf_op jit(solution)/shard_map/ppermute | solution.py:19
  83.6 1.7 %collective-permute-start.1 = (f32[256]{0:T(256)S(1)}, f32[256]{0:T(256)S(1)}, u32[]{:S(2)}, u32[]{:S(2)}) collective-permute-start(f32[256]{0:T(256)S(1)} %bitcast.76), channel_id=1, source_target_pairs={{0,4},{2,6},{4,0},{6,2},{8,12},{10,14},{12,8},{14,10},{16,20},{18,... | collective-permute-start | bytes 3080 | tf_op jit(solution)/shard_map/ppermute | solution.py:19
  85.3 3.3 %all-reduce.15 = f32[2560]{0:T(1024)S(1)} all-reduce(f32[2560]{0:T(1024)S(1)} %broadcast_select_fusion), channel_id=2, replica_groups=mesh['dp'=16,'head'=2] {'head'}, use_global_device_ids=true, to_apply=%region_2.3.clone | all-reduce | flops 2560 | bytes 20480
  91.8 1.6 %collective-permute-start.2 = (f32[256]{0:T(256)S(1)}, f32[256]{0:T(256)S(1)}, u32[]{:S(2)}, u32[]{:S(2)}) collective-permute-start(f32[256]{0:T(256)S(1)} %bitcast.78), channel_id=1, source_target_pairs={{0,8},{2,10},{4,12},{6,14},{8,0},{10,2},{12,4},{14,6},{16,24},{18,... | collective-permute-start | bytes 3080 | tf_op jit(solution)/shard_map/ppermute | solution.py:19
  96.6 2.5 %collective-permute-start.3 = (f32[256]{0:T(256)S(1)}, f32[256]{0:T(256)S(1)}, u32[]{:S(2)}, u32[]{:S(2)}) collective-permute-start(f32[256]{0:T(256)S(1)} %bitcast.77), channel_id=1, source_target_pairs={{0,16},{2,18},{4,20},{6,22},{8,24},{10,26},{12,28},{14,30},{16,0},... | collective-permute-start | bytes 3080 | tf_op jit(solution)/shard_map/ppermute | solution.py:19
  99.8 38.4 %all-reduce.16 = (f32[]{:T(128)}, f32[]{:T(128)}) all-reduce(f32[]{:T(128)} %get-tuple-element.723, f32[]{:T(128)} %get-tuple-element.713), channel_id=1, replica_groups=mesh['dp'=16,'head'=2] {'dp','head'}, use_global_device_ids=true, to_apply=%region_30.31 | all-reduce | flops 2 | bytes 16 | tf_op jit(solution)/shard_map/psum | solution.py:120
  (61 shorter events, 21.9 us)
Async XLA Ops:
  7.2 61.6 %copy-start = (bf16[2560,312]{0,1:T(8,128)(2,1)S(1)}, bf16[2560,312]{0,1:T(8,128)(2,1)}, u32[]{:S(2)}) copy-start(bf16[2560,312]{0,1:T(8,128)(2,1)} %param.30) | copy-start | bytes 4792324
  7.2 69.4 %reduce-scatter.2.cloned.1.call-start = ((), (), s32[]{:S(2)}) async-start(), calls=%async_computation.1 | async-start | bytes 7864320 | tf_op jit(solution)/shard_map/reduce_scatter | solution.py:79
  12.1 2.4 %copy-start.6 = (bf16[2560,156]{0,1:T(8,128)(2,1)S(1)}, bf16[2560,156]{0,1:T(8,128)(2,1)}, u32[]{:S(2)}) copy-start(bf16[2560,156]{0,1:T(8,128)(2,1)} %get-tuple-element.632) | copy-start | bytes 2396164 | tf_op jit(solution)/shard_map/cond
  20.6 2.4 %copy-start.1 = (bf16[2560,156]{0,1:T(8,128)(2,1)S(1)}, bf16[2560,156]{0,1:T(8,128)(2,1)}, u32[]{:S(2)}) copy-start(bf16[2560,156]{0,1:T(8,128)(2,1)} %param.34) | copy-start | bytes 2396164
  20.6 2.4 %copy-start.3 = (bf16[2560,156]{0,1:T(8,128)(2,1)S(1)}, bf16[2560,156]{0,1:T(8,128)(2,1)}, u32[]{:S(2)}) copy-start(bf16[2560,156]{0,1:T(8,128)(2,1)} %param.35) | copy-start | bytes 2396164
  61.7 4.5 %copy-start.8 = (s32[4,16]{1,0:T(4,128)S(1)}, s32[4,16]{1,0:T(4,128)}, u32[]{:S(2)}) copy-start(s32[4,16]{1,0:T(4,128)} %param.37) | copy-start | bytes 772
  61.7 7.1 %copy-start.10 = (bf16[312,512]{1,0:T(8,128)(2,1)S(1)}, bf16[312,512]{1,0:T(8,128)(2,1)}, u32[]{:S(2)}) copy-start(bf16[312,512]{1,0:T(8,128)(2,1)} %param.31) | copy-start | bytes 958468
  73.0 16.8 %copy-start.11 = (u32[32]{0:T(128)S(1)}, u32[32]{0:T(128)}, u32[]{:S(2)}) copy-start(u32[32]{0:T(128)} %constant.283) | copy-start | bytes 388
  73.1 26.0 %copy-start.9 = (s32[80]{0:T(128)S(1)}, s32[80]{0:T(128)}, u32[]{:S(2)}) copy-start(s32[80]{0:T(128)} %param.36) | copy-start | bytes 964
  79.8 3.8 %collective-permute-start = (f32[256]{0:T(256)S(1)}, f32[256]{0:T(256)S(1)}, u32[]{:S(2)}, u32[]{:S(2)}) collective-permute-start(f32[256]{0:T(256)S(1)} %bitcast.79), channel_id=1, source_target_pairs={{0,2},{2,0},{4,6},{6,4},{8,10},{10,8},{12,14},{14,12},{16,18},{18,... | collective-permute-start | bytes 3080 | tf_op jit(solution)/shard_map/ppermute | solution.py:19
  83.6 8.2 %collective-permute-start.1 = (f32[256]{0:T(256)S(1)}, f32[256]{0:T(256)S(1)}, u32[]{:S(2)}, u32[]{:S(2)}) collective-permute-start(f32[256]{0:T(256)S(1)} %bitcast.76), channel_id=1, source_target_pairs={{0,4},{2,6},{4,0},{6,2},{8,12},{10,14},{12,8},{14,10},{16,20},{18,... | collective-permute-start | bytes 3080 | tf_op jit(solution)/shard_map/ppermute | solution.py:19
  91.8 4.7 %collective-permute-start.2 = (f32[256]{0:T(256)S(1)}, f32[256]{0:T(256)S(1)}, u32[]{:S(2)}, u32[]{:S(2)}) collective-permute-start(f32[256]{0:T(256)S(1)} %bitcast.78), channel_id=1, source_target_pairs={{0,8},{2,10},{4,12},{6,14},{8,0},{10,2},{12,4},{14,6},{16,24},{18,... | collective-permute-start | bytes 3080 | tf_op jit(solution)/shard_map/ppermute | solution.py:19
  96.6 44.2 %collective-permute-start.3 = (f32[256]{0:T(256)S(1)}, f32[256]{0:T(256)S(1)}, u32[]{:S(2)}, u32[]{:S(2)}) collective-permute-start(f32[256]{0:T(256)S(1)} %bitcast.77), channel_id=1, source_target_pairs={{0,16},{2,18},{4,20},{6,22},{8,24},{10,26},{12,28},{14,30},{16,0},... | collective-permute-start | bytes 3080 | tf_op jit(solution)/shard_map/ppermute | solution.py:19
  140.9 0.6 copy-start.7
Sparse Core Ops, SparseCore 0:
  61.7 14.8 reduce-scatter.1
where the time goes:
time: 150 us; the launch traced here: 149 us
  blocking collectives  41.7 us (28%)
  local copies, waits for them, and re-layouts  36.1 us (24%)
  between operations  29.5 us (20%)
  matrix products  21.7 us (14%)
  other arithmetic  9.09 us (6%)
  starting transfers between devices  7.57 us (5%)
  waiting for transfers between devices  3.57 us (2%)
    psum x1, blocking collectives, body(): lax.psum((hidden_local, attention_local), ('dp', 'head'))  38.4 us
    another operation x10, local copies, waits for them, and re-layouts  15 us
    unnamed x22, local copies, waits for them, and re-layouts  14.9 us
    dot_general x5, matrix products, branch(): jnp.einsum('ic,jc->ij', teach_query[:used_rows], teach_key[:used_rows], p...  10.9 us
    ppermute x4, starting transfers between devices, partner(): return lax.ppermute(value, axis, pairs)  7.53 us
    dot_general x5, matrix products, branch(): jnp.einsum('ic,jc->ij', pupil_query[:used_rows], pupil_key[:used_rows], p...  6.59 us
    another operation x3, local copies, waits for them, and re-layouts, attention_rows(): jnp.stack([slot_map(tuple((member[slot_number] for member in pieces)), sl...  4.54 us
    dot_general x1, matrix products, body(): jnp.dot(student_hidden, projector, preferred_element_type=jnp.float32)  4.22 us
  transfers between devices with their start and end apart: 5, of which 1 were waited for; matrix products, arithmetic and copies ran while one was open for 8% of the time, Pallas kernels for 0%

commit v1 on v0

v1 whole, which is shorter than its diff:
```python
import functools
import math

import jax
import jax.numpy as jnp
from jax import lax
from jax.experimental import pallas as pl
from jax.experimental.pallas import tpu as pltpu
from jax.sharding import PartitionSpec as P

HEADS_T = 16
HEAD_T = 64
HEADS_S = 12
HEAD_S = 26
MESH = pl.DeviceIdType.MESH
NT = (((1,), (1,)), ((), ()))


def kernel(
    device_count, slots, rounds, width,
    th, sh, pj, tq, tk, sq, sk, lens, plan,
    hid_out, row_out, loss_out,
    thv, shv, pjv, tqv, tkv, sqv, skv,
    send, own, recv, hpart, hrecv, gath, tots,
    in_sem, pj_sem, x_send, x_recv, h_send, h_recv, g_send, g_recv, t_send, t_recv,
):
    me = lax.axis_index("dp")
    head = lax.axis_index("head")
    other = 1 - head
    tokens = tqv.shape[1]
    half = tokens // 2
    t_scale = 1.0 / (HEADS_T * math.sqrt(HEAD_T))
    s_scale = 1.0 / (HEADS_S * math.sqrt(HEAD_S))

    def fetch(index, source, target, slot):
        return pltpu.make_async_copy(
            source.at[pl.ds(slot * tokens, tokens), :], target.at[slot], in_sem.at[index, slot]
        )

    attend = ((tk, tkv), (tq, tqv), (sk, skv), (sq, sqv))
    hidden = ((sh, shv), (th, thv))

    @pl.loop(0, slots)
    def _(slot):
        for index, (source, target) in enumerate(attend):
            fetch(index, source, target, slot).start()

    pltpu.make_async_copy(pj, pjv, pj_sem).start()

    @pl.loop(0, slots)
    def _(slot):
        for index, (source, target) in enumerate(hidden):
            fetch(4 + index, source, target, slot).start()

    barrier = pltpu.get_barrier_semaphore()
    pl.semaphore_signal(barrier, inc=1, device_id=(me, other), device_id_type=MESH)

    @pl.loop(1, device_count)
    def _(step):
        peer = lax.rem(me + step, device_count)
        pl.semaphore_signal(barrier, inc=1, device_id=(peer, head), device_id_type=MESH)
        pl.semaphore_signal(barrier, inc=1, device_id=(peer, other), device_id_type=MESH)

    def exchange(slot):
        return pltpu.make_async_remote_copy(
            src_ref=send.at[slot], dst_ref=recv.at[slot],
            send_sem=x_send.at[slot], recv_sem=x_recv.at[slot],
            device_id=(me, other), device_id_type=MESH,
        )

    @pl.loop(0, slots)
    def _(slot):
        for index, (source, target) in enumerate(attend):
            fetch(index, source, target, slot).wait()

        def scores(which):
            rows = pl.ds(pl.multiple_of(which * half, half), half)
            teach = lax.dot_general(
                tkv[slot], tqv[slot, rows, :], NT, preferred_element_type=jnp.float32
            )
            pupil = lax.dot_general(
                skv[slot], sqv[slot, rows, :], NT, preferred_element_type=jnp.float32
            )
            return teach - pupil * (s_scale / t_scale)

        send[slot] = scores(other)
        own[slot] = scores(head)

        @pl.when(slot == 0)
        def _():
            pl.semaphore_wait(barrier, 2 * device_count - 1)

        exchange(slot).start()

    pltpu.make_async_copy(pj, pjv, pj_sem).wait()
    lanes = lax.broadcasted_iota(jnp.int32, (1, tokens), 1)

    @pl.loop(0, slots)
    def _(slot):
        for index, (source, target) in enumerate(hidden):
            fetch(4 + index, source, target, slot).wait()
        projected = jnp.dot(shv[slot], pjv[...], preferred_element_type=jnp.float32)
        errors = projected - thv[slot].astype(jnp.float32)
        squares = errors * errors
        folded = squares[:, :128]
        for start in range(128, squares.shape[1], 128):
            folded = folded + squares[:, start : start + 128]
        sums = jnp.sum(folded.T, axis=0, keepdims=True)
        sums = jnp.where(lanes < lens[me * slots + slot], sums, 0.0)
        hpart[2 * slot] = sums[:, :half]
        hpart[2 * slot + 1] = sums[:, half:]

    def add_length(index, sums):
        length = lens[index]
        return sums[0] + length, sums[1] + length * length

    total, total_sq = lax.fori_loop(
        0, device_count * slots, add_length, (jnp.int32(0), jnp.int32(0)), unroll=slots
    )

    owners = []
    for slot in range(slots):
        device, place = me, jnp.int32(slot)
        for bit in reversed(range(rounds)):
            mate = device ^ (2**bit)
            gave = plan[bit, device] == place
            place = jnp.where(gave, plan[bit, mate], place)
            device = jnp.where(gave, mate, device)
        owners.append((device, place))

    hidden_copy = pltpu.make_async_remote_copy(
        src_ref=hpart.at[pl.ds(other * slots, slots)], dst_ref=hrecv,
        send_sem=h_send, recv_sem=h_recv,
        device_id=(me, other), device_id_type=MESH,
    )
    hidden_copy.start()

    queries = lax.broadcasted_iota(jnp.int32, (1, half), 1) + head * half

    def reduce_slot(slot, totals):
        exchange(slot).wait_recv()
        length = lens[me * slots + slot]
        difference = own[slot] + recv[slot]
        keys = lax.broadcasted_iota(jnp.int32, (tokens, half), 0)
        squares = jnp.where(keys < length, difference * difference, 0.0)
        sums = jnp.sum(squares, axis=0, keepdims=True)
        sums = jnp.where(queries < length, sums * (t_scale * t_scale), 0.0)
        gath[me, slot] = sums / length.astype(jnp.float32)
        return totals + sums

    attention = lax.fori_loop(0, slots, reduce_slot, jnp.zeros((1, half), jnp.float32))

    hidden_copy.wait_recv()
    hidden_sum = jnp.zeros((1, half), jnp.float32)
    for row in range(slots):
        value = (hpart[head * slots + row] + hrecv[row]) / width
        for part in range(half // 128):
            index = row * (half // 128) + part
            hid_out[index : index + 1, :] = value[:, part * 128 : (part + 1) * 128]
        hidden_sum = hidden_sum + value
    gath[me, slots] = hidden_sum / total.astype(jnp.float32) + attention / total_sq.astype(
        jnp.float32
    )

    def rows_copy(step, source):
        return pltpu.make_async_remote_copy(
            src_ref=gath.at[source], dst_ref=gath.at[source],
            send_sem=g_send.at[step], recv_sem=g_recv.at[step],
            device_id=(lax.rem(me + step, device_count), head), device_id_type=MESH,
        )

    def total_copy(step, source):
        return pltpu.make_async_remote_copy(
            src_ref=gath.at[source, slots], dst_ref=tots.at[source],
            send_sem=t_send.at[step], recv_sem=t_recv.at[step],
            device_id=(lax.rem(me + step, device_count), other), device_id_type=MESH,
        )

    @pl.loop(1, device_count)
    def _(step):
        rows_copy(step, me).start()
        total_copy(step, me).start()

    total_copy(0, me).start()

    @pl.loop(0, slots)
    def _(slot):
        exchange(slot).wait_send()

    hidden_copy.wait_send()
    total_copy(0, me).wait_recv()

    @pl.loop(1, device_count)
    def _(step):
        source = lax.rem(me + device_count - step, device_count)
        rows_copy(step, source).wait_recv()
        total_copy(step, source).wait_recv()

    for slot, (device, place) in enumerate(owners):
        row_out[slot : slot + 1, :] = gath[device, place]
    pieces = jnp.sum(gath[:, slots], axis=0) + jnp.sum(tots[...], axis=0)
    loss_out[0, 0] = jnp.sum(pieces)

    total_copy(0, me).wait_send()

    @pl.loop(1, device_count)
    def _(step):
        rows_copy(step, me).wait_send()
        total_copy(step, me).wait_send()


def body(device_count, width, *operands):
    teacher_hidden, student_hidden, projector, _, _, student_queries, _, lengths, plan = operands
    slots = lengths.shape[0] // device_count
    tokens = teacher_hidden.shape[0] // slots
    half = tokens // 2
    cols_t = teacher_hidden.shape[1]
    cols_h = student_hidden.shape[1]
    cols_s = student_queries.shape[1]
    bf16, f32 = jnp.bfloat16, jnp.float32
    dma = pltpu.SemaphoreType.DMA
    anywhere = pl.BlockSpec(memory_space=pl.ANY)
    smem = pl.BlockSpec(memory_space=pltpu.SMEM)
    vmem = pl.BlockSpec(memory_space=pltpu.VMEM)
    hidden_row, row_loss, loss = pl.pallas_call(
        functools.partial(kernel, device_count, slots, plan.shape[0], width),
        out_shape=(
            jax.ShapeDtypeStruct((slots * half // 128, 128), f32),
            jax.ShapeDtypeStruct((slots, half), f32),
            jax.ShapeDtypeStruct((1, 1), f32),
        ),
        in_specs=[anywhere] * 7 + [smem] * 2,
        out_specs=(vmem, vmem, smem),
        scratch_shapes=[
            pltpu.VMEM((slots, tokens, cols_t), bf16),
            pltpu.VMEM((slots, tokens, cols_h), bf16),
            pltpu.VMEM(projector.shape, bf16),
            pltpu.VMEM((slots, tokens, cols_t), bf16),
            pltpu.VMEM((slots, tokens, cols_t), bf16),
            pltpu.VMEM((slots, tokens, cols_s), bf16),
            pltpu.VMEM((slots, tokens, cols_s), bf16),
            pltpu.VMEM((slots, tokens, half), f32),
            pltpu.VMEM((slots, tokens, half), f32),
            pltpu.VMEM((slots, tokens, half), f32),
            pltpu.VMEM((2 * slots, 1, half), f32),
            pltpu.VMEM((slots, 1, half), f32),
            pltpu.VMEM((device_count, slots + 1, 1, half), f32),
            pltpu.VMEM((device_count, 1, half), f32),
            dma((6, slots)),
            dma,
            dma((slots,)),
            dma((slots,)),
            dma,
            dma,
            dma((device_count,)),
            dma((device_count,)),
            dma((device_count,)),
            dma((device_count,)),
        ],
        compiler_params=pltpu.CompilerParams(
            collective_id=0, has_side_effects=True, vmem_limit_bytes=60 * 1024 * 1024
        ),
    )(*operands)
    return (
        hidden_row.reshape(slots * half),
        row_loss.reshape(1, 1, slots, half),
        loss.reshape(()),
    )


def solution(mesh):
    placed = (
        P("dp", "head"),
        P("dp", None),
        P(None, "head"),
        P("dp", "head"),
        P("dp", "head"),
        P("dp", "head"),
        P("dp", "head"),
        P(),
        P(),
    )

    def whole(*operands):
        width = operands[0].shape[1]
        return jax.shard_map(
            functools.partial(body, mesh.shape["dp"], width),
            mesh=mesh,
            in_specs=placed,
            out_specs=(P(("dp", "head")), P("dp", "head", None, None), P()),
            check_vma=False,
        )(*operands)

    return whole
```

time: 150 us -> 31.1 us (0.21)
  blocking collectives: 41.7 us -> 0 us
  local copies, waits for them, and re-layouts: 36.1 us -> 8.92 us
  between operations: 29.5 us -> 2.42 us
  matrix products: 21.7 us -> 0 us
  Pallas kernels: 0 us -> 19.4 us
  other arithmetic: 9.09 us -> 0 us
  starting transfers between devices: 7.57 us -> 0 us
  waiting for transfers between devices: 3.57 us -> 0 us
    psum x1 -> x0, blocking collectives: 38.4 us -> none  [body(): lax.psum((hidden_local, attention_local), ('dp', 'head'))]
    dot_general x11 -> x0, matrix products: 21.7 us -> none  [the longest x5 10.9 us: branch(): jnp.einsum('ic,jc->ij', teach_query[:used_rows], teach_key[:used_rows], p...]
    another operation x13 -> x0, local copies, waits for them, and re-layouts: 19.5 us -> none
    pallas_call x0 -> x1, Pallas kernels: none -> 19.4 us  [body(): pl.pallas_call(functools.partial(kernel, device_count, slots, plan.shape[...]
    ppermute x4 -> x0, starting transfers between devices: 7.53 us -> none  [partner(): return lax.ppermute(value, axis, pairs)]
    unnamed x22 -> x9, local copies, waits for them, and re-layouts: 14.9 us -> 8.92 us
    reduce_sum x5 -> x0, other arithmetic: 5.8 us -> none  [the longest x1 3.07 us: attention_rows(): return (row_losses, jnp.sum(squares))]
    reduce_scatter x1 -> x0, waiting for transfers between devices: 3.54 us -> none  [attention_rows(): lax.psum_scatter(full_maps, 'head', scatter_dimension=1, tiled=True)]
  transfers between devices with their start and end apart: 5 -> 0, of which waited for: 1 -> 0; matrix products, arithmetic and copies ran while one was open for 8% -> 0% of each run, Pallas kernels for 0% -> 0%
where the time goes in v1:
time: 31.1 us; the launch traced here: 30.8 us
  Pallas kernels  19.4 us (62%)
  local copies, waits for them, and re-layouts  8.92 us (29%)
  between operations  2.42 us (8%)
    pallas_call x1, Pallas kernels, body(): pl.pallas_call(functools.partial(kernel, device_count, slots, plan.shape[...  19.4 us
    unnamed x9, local copies, waits for them, and re-layouts  8.92 us

profile of v1, /device:TPU:0, one launch (start us, length us, event | category | flops | bytes accessed | tf_op | source)
XLA Modules:
  0.0 30.8 jit_solution(12142230226863001774)
XLA Ops:
  0.6 0.0 copy-start.1
  0.6 0.0 copy-start
  0.7 2.5 %copy.13.sq = bf16[2560,156]{1,0:T(8,128)(2,1)} copy(bf16[2560,156]{0,1:T(8,128)(2,1)} %param.14) | data formatting | bytes 1597440 | tf_op args[5]
  3.2 0.0 copy-done.1
  3.2 1.4 %copy.14.sk = bf16[2560,156]{1,0:T(8,128)(2,1)} copy(bf16[2560,156]{0,1:T(8,128)(2,1)S(1)} %copy-done.1) | data formatting | bytes 1597440 | tf_op args[6]
  4.5 0.0 copy-done
  4.5 2.4 %copy.12.sh = bf16[2560,312]{1,0:T(8,128)(2,1)} copy(bf16[2560,312]{0,1:T(8,128)(2,1)S(1)} %copy-done) | data formatting | bytes 3194880 | tf_op args[1]
  7.0 19.4 %shard_map.112 = (f32[10,128]{1,0:T(8,128)}, f32[5,256]{1,0:T(8,128)}, f32[1,1]{1,0:T(1,128)}) custom-call(bf16[2560,512]{1,0:T(8,128)(2,1)} %th.1, bf16[2560,312]{1,0:T(8,128)(2,1)} %copy.12.sh, bf16[312,512]{1,0:T(8,128)(2,1)} %pj.1, bf16[2560,512]{1,0:T(8,128)(2,1)} %tq.1, bf16[2560,512]{1,0:T(8,128)(2,1)} %tk.1, bf16[2560,156]{1,0:T(8,128)(2,1)} %copy.13.sq, ...), custom_call_target="tpu_custom_call" | custom-call | tf_op jit(solution)/shard_map/pallas_call | solution.py:225
  26.4 1.3 %copy.15 = f32[1,1,5,256]{3,1,2,0:T(1,128)} copy(f32[1,1,5,256]{3,2,1,0:T(8,128)} %bitcast.4) | data formatting | bytes 10240
  27.7 1.3 %copy.18 = f32[1280]{0:T(1024)} copy(f32[1280]{0:T(1024)} %bitcast.3) | data formatting | bytes 10240
Async XLA Ops:
  0.6 2.5 %copy-start.1 = (bf16[2560,156]{0,1:T(8,128)(2,1)S(1)}, bf16[2560,156]{0,1:T(8,128)(2,1)}, u32[]{:S(2)}) copy-start(bf16[2560,156]{0,1:T(8,128)(2,1)} %param.15) | copy-start | bytes 2396164
  0.6 3.9 %copy-start = (bf16[2560,312]{0,1:T(8,128)(2,1)S(1)}, bf16[2560,312]{0,1:T(8,128)(2,1)}, u32[]{:S(2)}) copy-start(bf16[2560,312]{0,1:T(8,128)(2,1)} %param.10) | copy-start | bytes 4792324

commit v2 on v1

v2 whole, which is shorter than its diff:
```python
import functools
import math

import jax
import jax.numpy as jnp
from jax import lax
from jax.experimental import pallas as pl
from jax.experimental.pallas import tpu as pltpu
from jax.sharding import PartitionSpec as P

HEADS_T = 16
HEAD_T = 64
HEADS_S = 12
HEAD_S = 26
MESH = pl.DeviceIdType.MESH
NT = (((1,), (1,)), ((), ()))
TN = (((0,), (0,)), ((), ()))


def kernel(
    device_count, slots, rounds, width,
    th, sh, pj, tq, tk, sq, sk, lens_hbm, plan_hbm,
    hid_out, row_out, loss_out,
    thv, shv, pjv, tqv, tkv, sqv, skv,
    lens, plan, totalv, send, own, recv, hpart, hrecv, gath, tots,
    in_sem, pj_sem, x_send, x_recv, h_send, h_recv, g_send, g_recv, t_send, t_recv, s_sem,
):
    me = lax.axis_index("dp")
    head = lax.axis_index("head")
    other = 1 - head
    tokens = tqv.shape[1]
    half = tokens // 2
    t_scale = 1.0 / (HEADS_T * math.sqrt(HEAD_T))
    s_scale = 1.0 / (HEADS_S * math.sqrt(HEAD_S))

    def fetch(index, source, target, slot):
        span = pl.ds(pl.multiple_of(slot * tokens, tokens), tokens)
        piece = source.at[:, span] if index in (2, 3, 4) else source.at[span, :]
        return pltpu.make_async_copy(piece, target.at[slot], in_sem.at[index, slot])

    attend = ((tk, tkv), (tq, tqv), (sk, skv), (sq, sqv))
    hidden = ((sh, shv), (th, thv))

    scalars = (
        pltpu.make_async_copy(lens_hbm, lens, s_sem.at[0]),
        pltpu.make_async_copy(plan_hbm, plan, s_sem.at[1]),
    )
    for copy in scalars:
        copy.start()
    for index, (source, target) in enumerate(attend):
        fetch(index, source, target, 0).start()

    barrier = pltpu.get_barrier_semaphore()
    pl.semaphore_signal(barrier, inc=1, device_id=(me, other), device_id_type=MESH)

    @pl.loop(1, device_count)
    def _(step):
        peer = lax.rem(me + step, device_count)
        pl.semaphore_signal(barrier, inc=1, device_id=(peer, head), device_id_type=MESH)
        pl.semaphore_signal(barrier, inc=1, device_id=(peer, other), device_id_type=MESH)

    @pl.loop(1, slots)
    def _(slot):
        for index, (source, target) in enumerate(attend):
            fetch(index, source, target, slot).start()

    pltpu.make_async_copy(pj, pjv, pj_sem).start()

    @pl.loop(0, slots)
    def _(slot):
        for index, (source, target) in enumerate(hidden):
            fetch(4 + index, source, target, slot).start()

    for copy in scalars:
        copy.wait()

    def add_length(index, sums):
        length = lens[index]
        return sums[0] + length, sums[1] + length * length

    total, total_sq = lax.fori_loop(
        0, device_count * slots, add_length, (jnp.int32(0), jnp.int32(0)), unroll=slots
    )

    owners = []
    for slot in range(slots):
        device, place = me, jnp.int32(slot)
        for bit in reversed(range(rounds)):
            mate = device ^ (2**bit)
            gave = plan[bit, device] == place
            place = jnp.where(gave, plan[bit, mate], place)
            device = jnp.where(gave, mate, device)
        owners.append((device, place))

    gate = min(2, slots - 1)

    def exchange(slot):
        return pltpu.make_async_remote_copy(
            src_ref=send.at[slot], dst_ref=recv.at[slot],
            send_sem=x_send, recv_sem=x_recv.at[slot],
            device_id=(me, other), device_id_type=MESH,
        )

    @pl.loop(0, slots)
    def _(slot):
        for index, (source, target) in enumerate(attend):
            fetch(index, source, target, slot).wait()

        def scores(which):
            rows = pl.ds(pl.multiple_of(which * half, half), half)
            teach = lax.dot_general(
                tkv[slot], tqv[slot, rows, :], NT, preferred_element_type=jnp.float32
            )
            pupil = lax.dot_general(
                skv[slot], sqv[slot, :, rows], TN, preferred_element_type=jnp.float32
            )
            return teach - pupil * (s_scale / t_scale)

        send[slot] = scores(other)
        own[slot] = scores(head)

        @pl.when(slot == gate)
        def _():
            pl.semaphore_wait(barrier, 2 * device_count - 1)

            @pl.loop(0, gate)
            def _(done):
                exchange(done).start()

        @pl.when(slot >= gate)
        def _():
            exchange(slot).start()

    def rows_copy(step):
        rows = gath.at[me]
        return pltpu.make_async_remote_copy(
            src_ref=rows, dst_ref=rows, send_sem=g_send, recv_sem=g_recv,
            device_id=(lax.rem(me + step, device_count), head), device_id_type=MESH,
        )

    def total_copy(step):
        return pltpu.make_async_remote_copy(
            src_ref=gath.at[me, slots], dst_ref=tots.at[me],
            send_sem=t_send, recv_sem=t_recv,
            device_id=(lax.rem(me + step, device_count), other), device_id_type=MESH,
        )

    queries = lax.broadcasted_iota(jnp.int32, (1, half), 1) + head * half
    totalv[...] = jnp.zeros_like(totalv)

    def reduce_slot(slot):
        exchange(slot).wait_recv()
        length = lens[me * slots + slot]
        difference = own[slot] + recv[slot]
        keys = lax.broadcasted_iota(jnp.int32, (tokens, half), 0)
        squares = jnp.where(keys < length, difference * difference, 0.0)
        sums = jnp.sum(squares, axis=0, keepdims=True)
        sums = jnp.where(queries < length, sums * (t_scale * t_scale), 0.0)
        gath[me, slot] = sums / length.astype(jnp.float32)
        totalv[...] += sums / total_sq.astype(jnp.float32)

    hidden_copy = pltpu.make_async_remote_copy(
        src_ref=hpart.at[pl.ds(other * slots, slots)], dst_ref=hrecv,
        send_sem=h_send, recv_sem=h_recv,
        device_id=(me, other), device_id_type=MESH,
    )
    pltpu.make_async_copy(pj, pjv, pj_sem).wait()
    lag = min(2, slots)
    lanes = lax.broadcasted_iota(jnp.int32, (1, tokens), 1)

    @pl.loop(0, slots)
    def _(slot):
        for index, (source, target) in enumerate(hidden):
            fetch(4 + index, source, target, slot).wait()
        projected = lax.dot_general(
            shv[slot], pjv[...], TN, preferred_element_type=jnp.float32
        )
        errors = projected - thv[slot].astype(jnp.float32)
        squares = errors * errors
        folded = squares[:, :128]
        for start in range(128, squares.shape[1], 128):
            folded = folded + squares[:, start : start + 128]
        sums = jnp.sum(folded.T, axis=0, keepdims=True)
        sums = jnp.where(lanes < lens[me * slots + slot], sums, 0.0)
        hpart[2 * slot] = sums[:, :half]
        hpart[2 * slot + 1] = sums[:, half:]
        totalv[...] += (sums[:, :half] + sums[:, half:]) / (width * total.astype(jnp.float32))

        @pl.when(slot >= lag)
        def _():
            reduce_slot(slot - lag)

    hidden_copy.start()

    @pl.loop(slots - lag, slots)
    def _(slot):
        reduce_slot(slot)

    gath[me, slots] = totalv[...]

    @pl.loop(1, device_count)
    def _(step):
        rows_copy(step).start()
        total_copy(step).start()

    total_copy(0).start()
    hidden_copy.wait_recv()
    for row in range(slots):
        value = (hpart[head * slots + row] + hrecv[row]) / width
        for part in range(half // 128):
            index = row * (half // 128) + part
            hid_out[index : index + 1, :] = value[:, part * 128 : (part + 1) * 128]


    others = gath.at[pl.ds(0, device_count - 1)]
    pltpu.make_async_copy(others, others, g_recv).wait()
    pltpu.make_async_copy(tots, tots, t_recv).wait()
    for slot, (device, place) in enumerate(owners):
        row_out[slot] = gath[device, place]
    pieces = jnp.sum(gath[:, slots], axis=0) + jnp.sum(tots[...], axis=0)
    loss_out[...] = jnp.sum(pieces, axis=1, keepdims=True)

    hidden_copy.wait_send()
    pltpu.make_async_copy(send, send, x_send).wait()
    pltpu.make_async_copy(others, others, g_send).wait()
    pltpu.make_async_copy(tots, tots, t_send).wait()


def hand_on(hid_in, row_in, loss_in, hid_out, row_out, loss_out):
    hid_out[...] = hid_in[...]
    row_out[...] = row_in[...]
    loss_out[...] = loss_in[...]


def body(device_count, width, *operands):
    teacher_hidden, student_hidden, projector, tq, tk, student_queries, sk, lengths, plan = operands
    slots = lengths.shape[0] // device_count
    tokens = teacher_hidden.shape[0] // slots
    half = tokens // 2
    cols_t = teacher_hidden.shape[1]
    cols_h = student_hidden.shape[1]
    cols_s = student_queries.shape[1]
    bf16, f32 = jnp.bfloat16, jnp.float32
    dma = pltpu.SemaphoreType.DMA
    anywhere = pl.BlockSpec(memory_space=pl.ANY)
    vmem = pl.BlockSpec(memory_space=pltpu.VMEM)
    hidden_row, row_loss, loss = pl.pallas_call(
        functools.partial(kernel, device_count, slots, plan.shape[0], width),
        out_shape=(
            jax.ShapeDtypeStruct((slots * half // 128, 128), f32),
            jax.ShapeDtypeStruct((slots, 1, half), f32),
            jax.ShapeDtypeStruct((1, 1), f32),
        ),
        in_specs=[anywhere] * 9,
        out_specs=(vmem, vmem, vmem),
        scratch_shapes=[
            pltpu.VMEM((slots, tokens, cols_t), bf16),
            pltpu.VMEM((slots, cols_h, tokens), bf16),
            pltpu.VMEM(projector.shape, bf16),
            pltpu.VMEM((slots, tokens, cols_t), bf16),
            pltpu.VMEM((slots, tokens, cols_t), bf16),
            pltpu.VMEM((slots, cols_s, tokens), bf16),
            pltpu.VMEM((slots, cols_s, tokens), bf16),
            pltpu.SMEM(lengths.shape, jnp.int32),
            pltpu.SMEM(plan.shape, jnp.int32),
            pltpu.VMEM((1, half), f32),
            pltpu.VMEM((slots, tokens, half), f32),
            pltpu.VMEM((slots, tokens, half), f32),
            pltpu.VMEM((slots, tokens, half), f32),
            pltpu.VMEM((2 * slots, 1, half), f32),
            pltpu.VMEM((slots, 1, half), f32),
            pltpu.VMEM((device_count, slots + 1, 1, half), f32),
            pltpu.VMEM((device_count, 1, half), f32),
            dma((6, slots)),
            dma,
            dma,
            dma((slots,)),
            dma,
            dma,
            dma,
            dma,
            dma,
            dma,
            dma((2,)),
        ],
        compiler_params=pltpu.CompilerParams(
            collective_id=0, has_side_effects=True, vmem_limit_bytes=60 * 1024 * 1024
        ),
    )(
        teacher_hidden, student_hidden.T, projector, tq, tk,
        student_queries.T, sk.T, lengths, plan,
    )
    hidden_row, row_loss, loss = pl.pallas_call(
        hand_on,
        out_shape=tuple(jax.ShapeDtypeStruct(x.shape, f32) for x in (hidden_row, row_loss, loss)),
        in_specs=(vmem, vmem, vmem),
        out_specs=(vmem, vmem, vmem),
    )(hidden_row, row_loss, loss)
    return (
        hidden_row.reshape(slots * half),
        row_loss.reshape(1, 1, slots, half),
        loss.reshape(()),
    )


def solution(mesh):
    placed = (
        P("dp", "head"),
        P("dp", None),
        P(None, "head"),
        P("dp", "head"),
        P("dp", "head"),
        P("dp", "head"),
        P("dp", "head"),
        P(),
        P(),
    )

    def whole(*operands):
        width = operands[0].shape[1]
        return jax.shard_map(
            functools.partial(body, mesh.shape["dp"], width),
            mesh=mesh,
            in_specs=placed,
            out_specs=(P(("dp", "head")), P("dp", "head", None, None), P()),
            check_vma=False,
        )(*operands)

    return whole
```

time: 31.1 us -> 20.3 us (0.65)
  local copies, waits for them, and re-layouts: 8.92 us -> 0 us
  between operations: 2.42 us -> 0.64 us
    unnamed x9 -> x0, local copies, waits for them, and re-layouts: 8.92 us -> none
    pallas_call x0 -> x1, Pallas kernels: none -> 1.92 us  [body(): pl.pallas_call(hand_on, out_shape=tuple((jax.ShapeDtypeStruct(x.shape, f3...]
    pallas_call x1, Pallas kernels: 19.4 us -> 17.5 us  [body(): pl.pallas_call(functools.partial(kernel, device_count, slots, plan.shape[...]
where the time goes in v2:
time: 20.3 us; the launch traced here: 20.1 us
  Pallas kernels  19.5 us (96%)
  between operations  0.64 us (3%)
    pallas_call x1, Pallas kernels, body(): pl.pallas_call(functools.partial(kernel, device_count, slots, plan.shape[...  17.5 us
    pallas_call x1, Pallas kernels, body(): pl.pallas_call(hand_on, out_shape=tuple((jax.ShapeDtypeStruct(x.shape, f3...  1.92 us

profile of v2, /device:TPU:0, one launch (start us, length us, event | category | flops | bytes accessed | tf_op | source)
XLA Modules:
  0.0 20.1 jit_solution(16140288245672517725)
XLA Ops:
  0.6 17.5 %shard_map.112 = (f32[10,128]{1,0:T(8,128)}, f32[5,1,256]{2,1,0:T(1,128)}, f32[1,1]{1,0:T(1,128)}) custom-call(bf16[2560,512]{1,0:T(8,128)(2,1)} %th.1, bf16[312,2560]{1,0:T(8,128)(2,1)} %bitcast.8, bf16[312,512]{1,0:T(8,128)(2,1)} %pj.1, bf16[2560,512]{1,0:T(8,128)(2,1)} %tq.1, bf16[2560,512]{1,0:T(8,128)(2,1)} %tk.1, bf16[156,2560]{1,0:T(8,128)(2,1)} %bitcast.9, ...), custom_call_target="tpu_custom_call" | custom-call | tf_op jit(solution)/shard_map/pallas_call | solution.py:247
  18.2 1.9 %shard_map.113 = (f32[10,128]{1,0:T(8,128)}, f32[5,1,256]{2,1,0:T(1,128)}, f32[1,1]{1,0:T(1,128)}) custom-call(f32[10,128]{1,0:T(8,128)} %get-tuple-element.9.hid_in, f32[5,1,256]{2,1,0:T(1,128)} %get-tuple-element.10.row_in, f32[1,1]{1,0:T(1,128)} %get-tuple-element.11.loss_in), custom_call_target="tpu_custom_call" | custom-call | tf_op jit(solution)/shard_map/pallas_call | solution.py:293
